TPU v7x, 512 devices: a whole 4x8x8 slice. The times are simulated.
512 devices in a mesh: dp: 64 (over y, x, core), mp: 8 (over z).
Axes of the slice: x: 4, y: 8, z: 8, core: 2. Of those that a mesh axis runs over, the one named last changes fastest.
Arguments:
- hidden: bfloat16 [960, 128, 2048], P('dp', None, 'mp'), may hold values from -6 to 6
- attn_out: bfloat16 [960, 128, 2048], P('dp', None, 'mp'), may hold values from -6 to 6
- out_proj: bfloat16 [2048, 2048], P(None, 'mp'), may hold values from -0.125 to 0.125
- norm_gain: float32 [2048], P('mp'), may hold values from 0.1 to 1.9
- reward_proj: float32 [2048, 8], P('mp'), may hold values from -0.125 to 0.125
- block_seq: int32 [960], replicated, may hold values from -1 to 383, as said below
- block_dest: int32 [960], replicated, may hold values from -1 to 639, as said below
- lengths: int32 [384], replicated, may hold values from 1 to 512, as said below
Outputs:
- token_rewards: float32 [640, 8, 128], P('dp')
- advantages: float32 [384], P('dp')
Inputs may be any that keep to these rules, and one draw needn't show every extreme that they name: `block_seq`: used slots of each index of dp come first in its 15 slots, the rest hold -1; each index of dp holds 1 to 15 used slots and some index holds exactly 15. Read over used slots in slot order, response numbers never fall, every response appears, and each has 1 to 4 blocks. `block_dest`: exactly the used slots (those of block_seq that are not -1) hold a destination; every owned slot of every owner is named exactly once, so each owner receives exactly 10 blocks; at most 1 block go from one index of dp to one owner, and that many in some pair. `lengths`: A response of n blocks has more than 128 * (n - 1) and at most 128 * n tokens.
All inputs are finite; a program needn't handle non-finite values.
Results may differ from a plain program's by a relative error of at most 0.0029.
Values may be sent and summed in bfloat16 or wider, within the bound.
No kernel may reach another device: no remote copies, remote signals or barrier semaphores. Data moves between devices by JAX's collectives and lax.ppermute only.
A program may use at most 64 MiB of HBM per device.

v0:
```python
import jax
import jax.numpy as jnp
from jax import lax
from jax.sharding import PartitionSpec as P

OWN_CAP = 10
norm_epsilon = 1e-05
stat_epsilon = 1e-06


def sent_to_all(value, axis):
    copies = jnp.broadcast_to(value, (lax.axis_size(axis), *value.shape))
    return lax.all_to_all(copies, axis, split_axis=0, concat_axis=0, tiled=True)


def of_everyone(value, axis):
    everything = sent_to_all(value, axis)
    return jnp.sum(everything, axis=0)


def packed_total(arrays, axis):
    ends = [0]
    for a in arrays:
        ends.append(ends[-1] + a.size)
    so_far = of_everyone(jnp.concatenate([a.ravel() for a in arrays]), axis)
    return tuple((so_far[b:e].reshape(a.shape) for a, b, e in zip(arrays, ends, ends[1:])))


def split_up(value, dim, peers):
    before, after = (value.shape[:dim], value.shape[dim + 1 :])
    return jnp.moveaxis(value.reshape(*before, peers, -1, *after), dim, 0)


def sent_and_summed(value, axis, dim):
    parts = split_up(value, dim, lax.axis_size(axis))
    arrived = lax.all_to_all(parts, axis, split_axis=0, concat_axis=0, tiled=True)
    return arrived.sum(axis=0)


def local(hidden, attn_out, out_proj, norm_gain, reward_proj, block_seq, block_dest, lengths):
    device_count = lax.axis_size("dp")
    device_rank = lax.axis_index("dp")
    slots_in = hidden.shape[0]
    block_len = hidden.shape[1]
    model_width = out_proj.shape[0]
    seq_count = lengths.shape[0]
    seq_local = seq_count // device_count
    slot_depth = (slots_in + device_count - 1) // device_count
    all_slots = jnp.arange(block_dest.shape[0], dtype=jnp.int32)
    local_dest = lax.dynamic_slice_in_dim(block_dest, device_rank * slots_in, slots_in)
    is_used = local_dest >= 0
    owner_rank = jnp.where(is_used, local_dest // OWN_CAP, -1)
    local_slots = jnp.arange(slots_in, dtype=jnp.int32)
    earlier = (
        (owner_rank[None, :] == owner_rank[:, None])
        & (local_slots[None, :] < local_slots[:, None])
        & is_used[None, :]
    )
    send_row = jnp.where(is_used, owner_rank * slot_depth + earlier.sum(axis=1), -1)
    buffer_rows = jnp.arange(device_count * slot_depth, dtype=jnp.int32)
    selector = (send_row[None, :] == buffer_rows[:, None]).astype(jnp.bfloat16)
    targets = device_rank * OWN_CAP + jnp.arange(OWN_CAP, dtype=jnp.int32)
    matches = block_dest[None, :] == targets[:, None]
    source_slot = jnp.sum(jnp.where(matches, all_slots[None, :], 0), axis=1)
    source_rank = source_slot // slots_in
    before = (block_dest[None, :] >= 0) & (block_dest[None, :] // OWN_CAP == device_rank)
    before = (
        before
        & (all_slots[None, :] >= (source_rank * slots_in)[:, None])
        & (all_slots[None, :] < source_slot[:, None])
    )
    recv_row = source_rank * slot_depth + before.sum(axis=1)
    seq_own = jnp.sum(jnp.where(matches, block_seq[None, :], 0), axis=1)
    earlier_same = (block_seq[None, :] == seq_own[:, None]) & (
        all_slots[None, :] < source_slot[:, None]
    )
    seq_rank = earlier_same.sum(axis=1)
    seq_ids = jnp.arange(seq_count, dtype=jnp.int32)
    member = seq_ids[:, None] == seq_own[None, :]
    own_length = jnp.sum(jnp.where(member, lengths[:, None], 0), axis=0)
    valid_tokens = jnp.minimum(block_len, own_length - block_len * seq_rank)
    projected = jnp.einsum(
        "btf,fc->btc",
        lax.all_gather(attn_out, "mp", axis=2, tiled=True),
        out_proj,
        preferred_element_type=jnp.float32,
    )
    local_resid = (hidden.astype(jnp.float32) + projected).astype(jnp.bfloat16)
    moved_resid = lax.all_to_all(
        jnp.einsum("rj,jtf->rtf", selector, local_resid, preferred_element_type=jnp.float32).astype(
            jnp.bfloat16
        ),
        "dp",
        split_axis=0,
        concat_axis=0,
        tiled=True,
    )
    residual = jnp.take(moved_resid, recv_row, axis=0)
    values = residual.astype(jnp.float32)
    squares = jnp.sum(values * values, axis=2)
    weighted = norm_gain[:, None] * reward_proj
    partial_value = jnp.einsum("btf,fh->bht", values, weighted, precision=lax.Precision.HIGHEST)
    squares, partial_value = packed_total((squares, partial_value), "mp")
    inverse_rms = lax.rsqrt(squares / model_width + norm_epsilon)
    live_tokens = (jnp.arange(block_len, dtype=jnp.int32)[None, :] < valid_tokens[:, None]).astype(
        jnp.float32
    )
    token_rewards = partial_value * (inverse_rms * live_tokens)[:, None, :]
    block_sums = jnp.sum(token_rewards, axis=2)
    seq_part = jnp.dot(member.astype(jnp.float32), block_sums, precision=lax.Precision.HIGHEST)
    seq_totals = sent_and_summed(seq_part, "dp", 0)
    own_lengths = lax.dynamic_slice_in_dim(lengths, device_rank * seq_local, seq_local).astype(
        jnp.float32
    )
    scores = seq_totals / own_lengths[:, None]
    worst_case = jnp.min(scores, axis=1)
    head_mean = jnp.mean(scores, axis=1)
    spread = jnp.mean((scores - head_mean[:, None]) ** 2, axis=1)
    total_seqs = float(seq_count)
    moment_sums = packed_total(
        (
            jnp.sum(spread),
            jnp.sum(worst_case),
            jnp.sum(worst_case * worst_case),
            jnp.sum(worst_case * spread),
            jnp.sum(spread * spread),
        ),
        "dp",
    )
    penalty_scale = moment_sums[0] / total_seqs + stat_epsilon
    conservative = worst_case - spread / penalty_scale
    first_sum = moment_sums[1] - moment_sums[0] / penalty_scale
    second = (
        moment_sums[2]
        - 2.0 * moment_sums[3] / penalty_scale
        + moment_sums[4] / (penalty_scale * penalty_scale)
    )
    centre = first_sum / total_seqs
    variance = second / total_seqs - centre * centre
    advantages = (conservative - centre) * lax.rsqrt(variance + stat_epsilon)
    return (token_rewards, advantages)


def solution(mesh):
    return jax.shard_map(
        local,
        mesh=mesh,
        in_specs=(
            P("dp", None, "mp"),
            P("dp", None, "mp"),
            P(None, "mp"),
            P("mp"),
            P("mp", None),
            P(),
            P(),
            P(),
        ),
        out_specs=(P("dp", None, None), P("dp")),
        check_vma=False,
    )
```

profile of v0, /device:TPU:1, one launch (start us, length us, event | category | flops | bytes accessed | tf_op | source)
XLA Modules:
  0.0 305.1 jit_solution(17338030331236136521)
XLA Ops:
  7.2 0.0 copy-start
  7.2 0.0 all-gather.2.cloned.1.call-start
  7.2 0.7 all-gather.2.cloned.1.call-update
  7.9 0.8 fusion.29
  8.7 0.2 convert_reduce_fusion.2
  8.9 101.2 %all-gather.2.cloned.1.call-done = bf16[15,128,2048]{2,1,0:T(8,128)(2,1)} async-done(((bf16[15,128,256]{2,1,0:T(8,128)(2,1)}), bf16[15,128,2048]{2,1,0:T(8,128)(2,1)}) %all-gather.2.cloned.1.call-update) | async-done | bytes 7864336 | tf_op jit(solution)/shard_map/all_gather | solution.py:84
  110.1 0.0 copy-done
  110.1 5.7 %add_convert_fusion = bf16[15,128,256]{2,1,0:T(8,128)(2,1)S(1)} fusion(bf16[15,128,256]{2,1,0:T(8,128)(2,1)} %param.8, bf16[15,128,2048]{2,1,0:T(8,128)(2,1)} %all-gather.2.cloned.1.call-done, bf16[2048,256]{1,0:T(8,128)(2,1)S(1)} %copy-done), kind=kOutput, calls=%fused_computation.3 | convolution fusion | flops 2014740480 | bytes 10878976 | tf_op jit(solution)/shard_map/btf,fc->btc/dot_general | solution.py:82
  115.8 1.4 convolution_convert_fusion
  117.1 4.4 %copy.29 = bf16[64,128,256]{2,1,0:T(8,128)(2,1)} copy(bf16[64,128,256]{2,0,1:T(8,128)(2,1)S(1)} %convolution_convert_fusion) | data formatting | bytes 8388608 | tf_op jit(solution)/shard_map/convert_element_type | solution.py:90
  121.5 0.0 copy-start.1
  121.5 0.0 copy-start.2
  121.5 0.0 copy-start.4
  121.5 0.0 copy-start.5
  121.5 13.3 %all-to-all-start = ((bf16[64,128,256]{2,1,0:T(8,128)(2,1)}), bf16[64,128,256]{2,1,0:T(8,128)(2,1)}, u32[]{:S(2)}, u32[]{:S(2)}) async-start(bf16[64,128,256]{2,1,0:T(8,128)(2,1)} %copy.29), calls=%async_computation | async-start | bytes 8388608 | tf_op jit(solution)/shard_map/all_to_all | solution.py:89
  134.8 0.0 copy-start.3
  134.9 0.0 copy-done.1
  134.9 0.0 copy-done.2
  134.9 0.2 fusion.3
  135.1 0.2 convert_reduce_fusion
  135.4 94.2 %all-to-all-done = bf16[64,128,256]{2,1,0:T(8,128)(2,1)} async-done(((bf16[64,128,256]{2,1,0:T(8,128)(2,1)}), bf16[64,128,256]{2,1,0:T(8,128)(2,1)}, u32[]{:S(2)}, u32[]{:S(2)}) %all-to-all-start) | async-done | bytes 4194336 | tf_op jit(solution)/shard_map/all_to_all | solution.py:89
  229.5 2.8 gather_fusion
  232.3 0.3 multiply_reduce_fusion
  232.7 0.0 copy-done.4
  232.7 0.0 copy-done.5
  232.7 0.7 convolution_bitcast_fusion
  233.4 0.9 broadcast_in_dim.89
  234.3 3.9 %all-to-all-start.1 = ((f32[8,1,11520]{2,1,0:T(1,128)}), f32[8,1,11520]{2,1,0:T(1,128)S(1)}, u32[]{:S(2)}, u32[]{:S(2)}) async-start(f32[8,1,11520]{2,1,0:T(1,128)} %broadcast_in_dim.89), calls=%async_computation.1 | async-start | bytes 737280 | tf_op jit(solution)/shard_map/all_to_all | solution.py:13
  238.2 0.0 copy-done.3
  238.2 0.2 select_reduce_fusion
  238.4 11.5 %all-to-all-done.1 = f32[8,1,11520]{2,1,0:T(1,128)S(1)} async-done(((f32[8,1,11520]{2,1,0:T(1,128)}), f32[8,1,11520]{2,1,0:T(1,128)S(1)}, u32[]{:S(2)}, u32[]{:S(2)}) %all-to-all-start.1) | async-done | bytes 368672 | tf_op jit(solution)/shard_map/all_to_all | solution.py:13
  249.9 0.3 reduce_sum.169
  250.2 0.1 fusion.15
  250.2 0.6 fusion.34
  250.9 0.2 fusion.7
  251.1 0.8 copy.32
  251.9 9.6 %all-to-all-start.2 = ((f32[64,6,8]{2,1,0:T(8,128)}), f32[64,6,8]{2,1,0:T(8,128)S(1)}, u32[]{:S(2)}, u32[]{:S(2)}) async-start(f32[64,6,8]{2,1,0:T(8,128)} %copy.32), calls=%async_computation.2 | async-start | bytes 524288 | tf_op jit(solution)/shard_map/all_to_all | solution.py:36
  261.6 0.1 dynamic-slice_convert_fusion
  261.6 13.0 %all-to-all-done.2 = f32[64,6,8]{2,1,0:T(8,128)S(1)} async-done(((f32[64,6,8]{2,1,0:T(8,128)}), f32[64,6,8]{2,1,0:T(8,128)S(1)}, u32[]{:S(2)}, u32[]{:S(2)}) %all-to-all-start.2) | async-done | bytes 12320 | tf_op jit(solution)/shard_map/all_to_all | solution.py:36
  274.6 0.1 reduce_sum.174
  274.7 0.2 fusion.32
  274.9 0.2 multiply_reduce_fusion.1
  275.1 0.7 multiply_reduce_fusion.2
  275.8 3.2 %concatenate.7 = f32[5]{0:T(128)S(1)} concatenate(f32[1]{0:T(128)} %bitcast.13, f32[1]{0:T(128)} %bitcast.14, f32[1]{0:T(128)} %bitcast.15, f32[1]{0:T(128)} %bitcast.16, f32[1]{0:T(128)} %bitcast.17), dimensions={0} | concatenate | bytes 40 | tf_op jit(solution)/shard_map/concatenate | solution.py:25
  279.1 14.0 %all_to_all.22 = f32[64,1,5]{2,1,0:T(1,128)S(1)} all-to-all(f32[64,1,5]{2,1,0:T(1,128)S(1)} %broadcast_in_dim.93), channel_id=1, replica_groups=mesh['dp'=64,'mp'=8] {'dp'}, dimensions={0} | all-to-all | bytes 2560 | tf_op jit(solution)/shard_map/all_to_all | solution.py:13
  293.1 0.1 reduce_sum.182
  293.1 0.7 fusion.36
  297.7 0.5 subtract_multiply_fusion
  (12 shorter events, 0.1 us)
Async XLA Ops:
  7.2 102.9 %copy-start = (bf16[2048,256]{1,0:T(8,128)(2,1)S(1)}, bf16[2048,256]{1,0:T(8,128)(2,1)}, u32[]{:S(2)}) copy-start(bf16[2048,256]{1,0:T(8,128)(2,1)} %param.10) | copy-start | bytes 3145732
  7.2 102.9 %all-gather.2.cloned.1.call-start = ((), (), s32[]{:S(2)}) async-start(), calls=%async_computation.4 | async-start | bytes 8847360 | tf_op jit(solution)/shard_map/all_gather | solution.py:84
  121.5 13.3 %copy-start.1 = (s32[960]{0:T(1024)S(1)}, s32[960]{0:T(1024)}, u32[]{:S(2)}) copy-start(s32[960]{0:T(1024)} %param.14) | copy-start | bytes 11524
  121.5 13.3 %copy-start.2 = (s32[960]{0:T(1024)S(1)}, s32[960]{0:T(1024)}, u32[]{:S(2)}) copy-start(s32[960]{0:T(1024)} %param.13) | copy-start | bytes 11524
  121.5 111.1 %copy-start.4 = (f32[256,8]{0,1:T(8,128)S(1)}, f32[256,8]{0,1:T(8,128)}, u32[]{:S(2)}) copy-start(f32[256,8]{0,1:T(8,128)} %param.12) | copy-start | bytes 24580
  121.5 111.1 %copy-start.5 = (f32[256]{0:T(256)S(1)}, f32[256]{0:T(256)}, u32[]{:S(2)}) copy-start(f32[256]{0:T(256)} %param.11) | copy-start | bytes 3076
  121.5 108.0 %all-to-all-start = ((bf16[64,128,256]{2,1,0:T(8,128)(2,1)}), bf16[64,128,256]{2,1,0:T(8,128)(2,1)}, u32[]{:S(2)}, u32[]{:S(2)}) async-start(bf16[64,128,256]{2,1,0:T(8,128)(2,1)} %copy.29), calls=%async_computation | async-start | bytes 8388608 | tf_op jit(solution)/shard_map/all_to_all | solution.py:89
  134.8 103.4 %copy-start.3 = (s32[384]{0:T(512)S(1)}, s32[384]{0:T(512)}, u32[]{:S(2)}) copy-start(s32[384]{0:T(512)} %param.15) | copy-start | bytes 4612
  234.3 15.6 %all-to-all-start.1 = ((f32[8,1,11520]{2,1,0:T(1,128)}), f32[8,1,11520]{2,1,0:T(1,128)S(1)}, u32[]{:S(2)}, u32[]{:S(2)}) async-start(f32[8,1,11520]{2,1,0:T(1,128)} %broadcast_in_dim.89), calls=%async_computation.1 | async-start | bytes 737280 | tf_op jit(solution)/shard_map/all_to_all | solution.py:13
  251.9 22.7 %all-to-all-start.2 = ((f32[64,6,8]{2,1,0:T(8,128)}), f32[64,6,8]{2,1,0:T(8,128)S(1)}, u32[]{:S(2)}, u32[]{:S(2)}) async-start(f32[64,6,8]{2,1,0:T(8,128)} %copy.32), calls=%async_computation.2 | async-start | bytes 524288 | tf_op jit(solution)/shard_map/all_to_all | solution.py:36
Sparse Core Ops, SparseCore 0:
  10.0 100.0 all-gather.1
where the time goes:
time: 306 us; the launch traced here: 305 us
  waiting for transfers between devices  221 us (72%)
  starting transfers between devices  26.8 us (9%)
  between operations  18.1 us (6%)
  blocking collectives  14 us (5%)
  local copies, waits for them, and re-layouts  12.9 us (4%)
  matrix products  7.93 us (3%)
  other arithmetic  4.83 us (2%)
    all_gather x1, waiting for transfers between devices, local(): lax.all_gather(attn_out, 'mp', axis=2, tiled=True)  101 us
    all_to_all x1, waiting for transfers between devices, local(): lax.all_to_all(jnp.einsum('rj,jtf->rtf', selector, local_resid, preferred...  94.2 us
    all_to_all x1, blocking collectives, sent_to_all(): return lax.all_to_all(copies, axis, split_axis=0, concat_axis=0, tiled=True)  14 us
    all_to_all x1, starting transfers between devices, local(): lax.all_to_all(jnp.einsum('rj,jtf->rtf', selector, local_resid, preferred...  13.3 us
    all_to_all x1, waiting for transfers between devices, sent_and_summed(): lax.all_to_all(parts, axis, split_axis=0, concat_axis=0, tiled=True)  13 us
    all_to_all x1, waiting for transfers between devices, sent_to_all(): return lax.all_to_all(copies, axis, split_axis=0, concat_axis=0, tiled=True)  11.5 us
    all_to_all x1, starting transfers between devices, sent_and_summed(): lax.all_to_all(parts, axis, split_axis=0, concat_axis=0, tiled=True)  9.64 us
  transfers between devices with their start and end apart: 4, of which 4 were waited for; matrix products, arithmetic and copies ran while one was open for 1% of the time, Pallas kernels for 0%

commit v1 on v0

--- a/solution.py
+++ b/solution.py
@@ -79,12 +79,37 @@
     member = seq_ids[:, None] == seq_own[None, :]
     own_length = jnp.sum(jnp.where(member, lengths[:, None], 0), axis=0)
     valid_tokens = jnp.minimum(block_len, own_length - block_len * seq_rank)
+    size, position, rows = (lax.axis_size("mp"), lax.axis_index("mp"), attn_out.shape[2])
+    right = [(i, (i + 1) % size) for i in range(size)]
+    left = [(i, (i - 1) % size) for i in range(size)]
+    halfway = size // 2
+    from_left = from_right = attn_out
     projected = jnp.einsum(
         "btf,fc->btc",
-        lax.all_gather(attn_out, "mp", axis=2, tiled=True),
-        out_proj,
+        attn_out,
+        lax.dynamic_slice_in_dim(out_proj, position * rows, attn_out.shape[2], axis=0),
         preferred_element_type=jnp.float32,
     )
+    for step in range(1, halfway + 1):
+        from_left = lax.ppermute(from_left, "mp", right)
+        if step < size - halfway:
+            from_right = lax.ppermute(from_right, "mp", left)
+            projected = projected + jnp.einsum(
+                "btf,fc->btc",
+                from_right,
+                lax.dynamic_slice_in_dim(
+                    out_proj, (position + step) % size * rows, from_right.shape[2], axis=0
+                ),
+                preferred_element_type=jnp.float32,
+            )
+        projected = projected + jnp.einsum(
+            "btf,fc->btc",
+            from_left,
+            lax.dynamic_slice_in_dim(
+                out_proj, (position - step) % size * rows, from_left.shape[2], axis=0
+            ),
+            preferred_element_type=jnp.float32,
+        )
     local_resid = (hidden.astype(jnp.float32) + projected).astype(jnp.bfloat16)
     moved_resid = lax.all_to_all(
         jnp.einsum("rj,jtf->rtf", selector, local_resid, preferred_element_type=jnp.float32).astype(

time: 306 us -> 294 us (0.961)
  waiting for transfers between devices: 221 us -> 185 us
  starting transfers between devices: 26.8 us -> 55.7 us
  between operations: 18.1 us -> 5.08 us
  matrix products: 7.93 us -> 11.6 us
  local copies, waits for them, and re-layouts: 12.9 us -> 16.3 us
    all_gather x1 -> x0, waiting for transfers between devices: 101 us -> none  [local(): lax.all_gather(attn_out, 'mp', axis=2, tiled=True)]
    ppermute x0 -> x7, waiting for transfers between devices: none -> 66.6 us  [the longest x4 66.6 us: local(): from_left = lax.ppermute(from_left, 'mp', right)]
    ppermute x0 -> x7, starting transfers between devices: none -> 28.4 us  [the longest x3 17.7 us: local(): from_right = lax.ppermute(from_right, 'mp', left)]
    dot_general x1 -> x8, matrix products: 5.65 us -> 9.31 us  [the longest x4 4.97 us: local(): jnp.einsum('btf,fc->btc', from_left, lax.dynamic_slice_in_dim(out_proj, (...]
  transfers between devices with their start and end apart: 4 -> 10, of which waited for: 4 -> 7; matrix products, arithmetic and copies ran while one was open for 1% -> 4% of each run, Pallas kernels for 0% -> 0%
where the time goes in v1:
time: 294 us; the launch traced here: 293 us
  waiting for transfers between devices  185 us (63%)
  starting transfers between devices  55.7 us (19%)
  local copies, waits for them, and re-layouts  16.3 us (6%)
  blocking collectives  14 us (5%)
  matrix products  11.6 us (4%)
  between operations  5.08 us (2%)
  other arithmetic  4.83 us (2%)
    all_to_all x1, waiting for transfers between devices, local(): lax.all_to_all(jnp.einsum('rj,jtf->rtf', selector, local_resid, preferred...  94.1 us
    ppermute x4, waiting for transfers between devices, local(): from_left = lax.ppermute(from_left, 'mp', right)  66.6 us
    ppermute x3, starting transfers between devices, local(): from_right = lax.ppermute(from_right, 'mp', left)  17.7 us
    all_to_all x1, starting transfers between devices, local(): lax.all_to_all(jnp.einsum('rj,jtf->rtf', selector, local_resid, preferred...  14.3 us
    all_to_all x1, blocking collectives, sent_to_all(): return lax.all_to_all(copies, axis, split_axis=0, concat_axis=0, tiled=True)  14 us
    all_to_all x1, waiting for transfers between devices, sent_and_summed(): lax.all_to_all(parts, axis, split_axis=0, concat_axis=0, tiled=True)  13 us
    all_to_all x1, waiting for transfers between devices, sent_to_all(): return lax.all_to_all(copies, axis, split_axis=0, concat_axis=0, tiled=True)  11.4 us
    ppermute x4, starting transfers between devices, local(): from_left = lax.ppermute(from_left, 'mp', right)  10.7 us
  transfers between devices with their start and end apart: 10, of which 7 were waited for; matrix products, arithmetic and copies ran while one was open for 4% of the time, Pallas kernels for 0%

profile of v1, /device:TPU:1, one launch (start us, length us, event | category | flops | bytes accessed | tf_op | source)
XLA Modules:
  0.0 292.6 jit_solution(2970092903370639773)
XLA Ops:
  0.7 4.9 %collective-permute-start.1 = (bf16[15,128,256]{2,1,0:T(8,128)(2,1)}, bf16[15,128,256]{2,1,0:T(8,128)(2,1)S(1)}, u32[]{:S(2)}, u32[]{:S(2)}) collective-permute-start(bf16[15,128,256]{2,1,0:T(8,128)(2,1)} %param.9), channel_id=1, source_target_pairs={{0,1},{1,2},{2,3},{3,4},{4,5},{5,6},{6,7},{7,0},{8,9},{9,10},{10,1... | collective-permute-start | bytes 2949128 | tf_op jit(solution)/shard_map/ppermute | solution.py:94
  5.6 8.6 %collective-permute-start = (bf16[15,128,256]{2,1,0:T(8,128)(2,1)}, bf16[15,128,256]{2,1,0:T(8,128)(2,1)}, u32[]{:S(2)}, u32[]{:S(2)}) collective-permute-start(bf16[15,128,256]{2,1,0:T(8,128)(2,1)} %param.9), channel_id=1, source_target_pairs={{0,7},{1,0},{2,1},{3,2},{4,3},{5,4},{6,5},{7,6},{8,15},{9,8},{10,9... | collective-permute-start | bytes 2949128 | tf_op jit(solution)/shard_map/ppermute | solution.py:96
  14.2 19.7 %collective-permute-done.1 = bf16[15,128,256]{2,1,0:T(8,128)(2,1)S(1)} collective-permute-done((bf16[15,128,256]{2,1,0:T(8,128)(2,1)}, bf16[15,128,256]{2,1,0:T(8,128)(2,1)S(1)}, u32[]{:S(2)}, u32[]{:S(2)}) %collective-permute-start.1) | collective-permute-done | bytes 983072 | tf_op jit(solution)/shard_map/ppermute | solution.py:94
  33.9 1.9 collective-permute-start.3
  35.9 4.6 %collective-permute-start.2 = (bf16[15,128,256]{2,1,0:T(8,128)(2,1)}, bf16[15,128,256]{2,1,0:T(8,128)(2,1)}, u32[]{:S(2)}, u32[]{:S(2)}) collective-permute-start(bf16[15,128,256]{2,1,0:T(8,128)(2,1)} %collective-permute-done), channel_id=1, source_target_pairs={{0,7},{1,0},{2,1},{3,2},{4,3},{5,4},{6,5},{7,6},{8,15},{9,8},{10,9... | collective-permute-start | bytes 2949128 | tf_op jit(solution)/shard_map/ppermute | solution.py:96
  40.5 0.8 fusion.59
  41.2 0.2 convert_reduce_fusion.2
  41.4 17.8 %collective-permute-done.3 = bf16[15,128,256]{2,1,0:T(8,128)(2,1)} collective-permute-done((bf16[15,128,256]{2,1,0:T(8,128)(2,1)S(1)}, bf16[15,128,256]{2,1,0:T(8,128)(2,1)}, u32[]{:S(2)}, u32[]{:S(2)}) %collective-permute-start.3) | collective-permute-done | bytes 983072 | tf_op jit(solution)/shard_map/ppermute | solution.py:94
  59.2 1.9 collective-permute-start.5
  61.3 1.6 copy.55
  62.9 0.5 fusion.14
  63.4 0.7 copy-done.3
  64.1 0.5 fusion.10
  64.6 4.6 %collective-permute-start.4 = (bf16[15,128,256]{2,1,0:T(8,128)(2,1)}, bf16[15,128,256]{2,1,0:T(8,128)(2,1)S(1)}, u32[]{:S(2)}, u32[]{:S(2)}) collective-permute-start(bf16[15,128,256]{2,1,0:T(8,128)(2,1)} %collective-permute-done.2), channel_id=1, source_target_pairs={{0,7},{1,0},{2,1},{3,2},{4,3},{5,4},{6,5},{7,6},{8,15},{9,8},{10,9... | collective-permute-start | bytes 2949128 | tf_op jit(solution)/shard_map/ppermute | solution.py:96
  69.2 1.7 fusion.12
  70.9 12.9 %collective-permute-done.5 = bf16[15,128,256]{2,1,0:T(8,128)(2,1)} collective-permute-done((bf16[15,128,256]{2,1,0:T(8,128)(2,1)}, bf16[15,128,256]{2,1,0:T(8,128)(2,1)}, u32[]{:S(2)}, u32[]{:S(2)}) %collective-permute-start.5) | collective-permute-done | bytes 983072 | tf_op jit(solution)/shard_map/ppermute | solution.py:94
  83.8 1.9 collective-permute-start.6
  85.7 1.7 fusion.6
  87.4 1.7 fusion.8
  89.1 1.7 fusion.2
  90.8 0.5 fusion.4
  91.3 16.2 %collective-permute-done.6 = bf16[15,128,256]{2,1,0:T(8,128)(2,1)S(1)} collective-permute-done((bf16[15,128,256]{2,1,0:T(8,128)(2,1)}, bf16[15,128,256]{2,1,0:T(8,128)(2,1)S(1)}, u32[]{:S(2)}, u32[]{:S(2)}) %collective-permute-start.6) | collective-permute-done | bytes 983072 | tf_op jit(solution)/shard_map/ppermute | solution.py:94
  107.5 1.1 fusion
  108.6 1.1 copy.64
  109.7 1.4 convolution_convert_fusion
  111.0 4.4 %copy.65 = bf16[64,128,256]{2,1,0:T(8,128)(2,1)} copy(bf16[64,128,256]{2,0,1:T(8,128)(2,1)S(1)} %convolution_convert_fusion) | data formatting | bytes 8388608 | tf_op jit(solution)/shard_map/convert_element_type | solution.py:115
  115.4 14.3 %all-to-all-start = ((bf16[64,128,256]{2,1,0:T(8,128)(2,1)}), bf16[64,128,256]{2,1,0:T(8,128)(2,1)}, u32[]{:S(2)}, u32[]{:S(2)}) async-start(bf16[64,128,256]{2,1,0:T(8,128)(2,1)} %copy.65), calls=%async_computation | async-start | bytes 8388608 | tf_op jit(solution)/shard_map/all_to_all | solution.py:114
  129.8 0.2 fusion.25
  130.0 0.2 convert_reduce_fusion
  130.3 94.1 %all-to-all-done = bf16[64,128,256]{2,1,0:T(8,128)(2,1)} async-done(((bf16[64,128,256]{2,1,0:T(8,128)(2,1)}), bf16[64,128,256]{2,1,0:T(8,128)(2,1)}, u32[]{:S(2)}, u32[]{:S(2)}) %all-to-all-start) | async-done | bytes 4194336 | tf_op jit(solution)/shard_map/all_to_all | solution.py:114
  224.4 2.8 gather_fusion
  227.2 0.3 multiply_reduce_fusion
  227.5 0.7 convolution_bitcast_fusion
  228.3 0.9 broadcast_in_dim.89
  229.2 3.6 %all-to-all-start.1 = ((f32[8,1,11520]{2,1,0:T(1,128)}), f32[8,1,11520]{2,1,0:T(1,128)S(1)}, u32[]{:S(2)}, u32[]{:S(2)}) async-start(f32[8,1,11520]{2,1,0:T(1,128)} %broadcast_in_dim.89), calls=%async_computation.1 | async-start | bytes 737280 | tf_op jit(solution)/shard_map/all_to_all | solution.py:13
  233.0 11.4 %all-to-all-done.1 = f32[8,1,11520]{2,1,0:T(1,128)S(1)} async-done(((f32[8,1,11520]{2,1,0:T(1,128)}), f32[8,1,11520]{2,1,0:T(1,128)S(1)}, u32[]{:S(2)}, u32[]{:S(2)}) %all-to-all-start.1) | async-done | bytes 368672 | tf_op jit(solution)/shard_map/all_to_all | solution.py:13
  244.5 0.3 reduce_sum.169
  244.8 0.6 fusion.64
  245.4 0.2 fusion.29
  245.6 0.8 copy.68
  246.5 9.4 %all-to-all-start.2 = ((f32[64,6,8]{2,1,0:T(8,128)}), f32[64,6,8]{2,1,0:T(8,128)S(1)}, u32[]{:S(2)}, u32[]{:S(2)}) async-start(f32[64,6,8]{2,1,0:T(8,128)} %copy.68), calls=%async_computation.2 | async-start | bytes 524288 | tf_op jit(solution)/shard_map/all_to_all | solution.py:36
  256.0 13.0 %all-to-all-done.2 = f32[64,6,8]{2,1,0:T(8,128)S(1)} async-done(((f32[64,6,8]{2,1,0:T(8,128)}), f32[64,6,8]{2,1,0:T(8,128)S(1)}, u32[]{:S(2)}, u32[]{:S(2)}) %all-to-all-start.2) | async-done | bytes 12320 | tf_op jit(solution)/shard_map/all_to_all | solution.py:36
  269.3 0.2 multiply_reduce_fusion.1
  269.5 0.7 multiply_reduce_fusion.2
  270.2 3.2 %concatenate.7 = f32[5]{0:T(128)S(1)} concatenate(f32[1]{0:T(128)} %bitcast.21, f32[1]{0:T(128)} %bitcast.22, f32[1]{0:T(128)} %bitcast.23, f32[1]{0:T(128)} %bitcast.24, f32[1]{0:T(128)} %bitcast.25), dimensions={0} | concatenate | bytes 40 | tf_op jit(solution)/shard_map/concatenate | solution.py:25
  273.4 14.0 %all_to_all.22 = f32[64,1,5]{2,1,0:T(1,128)S(1)} all-to-all(f32[64,1,5]{2,1,0:T(1,128)S(1)} %broadcast_in_dim.93), channel_id=1, replica_groups=mesh['dp'=64,'mp'=8] {'dp'}, dimensions={0} | all-to-all | bytes 2560 | tf_op jit(solution)/shard_map/all_to_all | solution.py:13
  287.5 0.7 fusion.66
  292.1 0.5 subtract_multiply_fusion
  (38 shorter events, 0.9 us)
Async XLA Ops:
  0.6 62.3 %copy-start = (bf16[2048,256]{1,0:T(8,128)(2,1)S(1)}, bf16[2048,256]{1,0:T(8,128)(2,1)}, u32[]{:S(2)}) copy-start(bf16[2048,256]{1,0:T(8,128)(2,1)} %param.10) | copy-start | bytes 3145732
  0.6 62.3 %copy-start.1 = (bf16[15,128,256]{2,1,0:T(8,128)(2,1)S(1)}, bf16[15,128,256]{2,1,0:T(8,128)(2,1)}, u32[]{:S(2)}) copy-start(bf16[15,128,256]{2,1,0:T(8,128)(2,1)} %param.9) | copy-start | bytes 2949124
  0.7 33.3 %collective-permute-start.1 = (bf16[15,128,256]{2,1,0:T(8,128)(2,1)}, bf16[15,128,256]{2,1,0:T(8,128)(2,1)S(1)}, u32[]{:S(2)}, u32[]{:S(2)}) collective-permute-start(bf16[15,128,256]{2,1,0:T(8,128)(2,1)} %param.9), channel_id=1, source_target_pairs={{0,1},{1,2},{2,3},{3,4},{4,5},{5,6},{6,7},{7,0},{8,9},{9,10},{10,1... | collective-permute-start | bytes 2949128 | tf_op jit(solution)/shard_map/ppermute | solution.py:94
  5.6 30.3 %collective-permute-start = (bf16[15,128,256]{2,1,0:T(8,128)(2,1)}, bf16[15,128,256]{2,1,0:T(8,128)(2,1)}, u32[]{:S(2)}, u32[]{:S(2)}) collective-permute-start(bf16[15,128,256]{2,1,0:T(8,128)(2,1)} %param.9), channel_id=1, source_target_pairs={{0,7},{1,0},{2,1},{3,2},{4,3},{5,4},{6,5},{7,6},{8,15},{9,8},{10,9... | collective-permute-start | bytes 2949128 | tf_op jit(solution)/shard_map/ppermute | solution.py:96
  33.9 27.3 %copy-start.2 = (bf16[15,128,256]{2,1,0:T(8,128)(2,1)}, bf16[15,128,256]{2,1,0:T(8,128)(2,1)S(1)}, u32[]{:S(2)}) copy-start(bf16[15,128,256]{2,1,0:T(8,128)(2,1)S(1)} %collective-permute-done.1) | copy-start | bytes 2949124
  33.9 25.3 %collective-permute-start.3 = (bf16[15,128,256]{2,1,0:T(8,128)(2,1)S(1)}, bf16[15,128,256]{2,1,0:T(8,128)(2,1)}, u32[]{:S(2)}, u32[]{:S(2)}) collective-permute-start(bf16[15,128,256]{2,1,0:T(8,128)(2,1)S(1)} %collective-permute-done.1), channel_id=1, source_target_pairs={{0,1},{1,2},{2,3},{3,4},{4,5},{5,6},{6,7},{7,0},{8,9},{9,10},{10,1... | collective-permute-start | bytes 2949128 | tf_op jit(solution)/shard_map/ppermute | solution.py:94
  35.9 28.8 %collective-permute-start.2 = (bf16[15,128,256]{2,1,0:T(8,128)(2,1)}, bf16[15,128,256]{2,1,0:T(8,128)(2,1)}, u32[]{:S(2)}, u32[]{:S(2)}) collective-permute-start(bf16[15,128,256]{2,1,0:T(8,128)(2,1)} %collective-permute-done), channel_id=1, source_target_pairs={{0,7},{1,0},{2,1},{3,2},{4,3},{5,4},{6,5},{7,6},{8,15},{9,8},{10,9... | collective-permute-start | bytes 2949128 | tf_op jit(solution)/shard_map/ppermute | solution.py:96
  59.2 24.6 %collective-permute-start.5 = (bf16[15,128,256]{2,1,0:T(8,128)(2,1)}, bf16[15,128,256]{2,1,0:T(8,128)(2,1)}, u32[]{:S(2)}, u32[]{:S(2)}) collective-permute-start(bf16[15,128,256]{2,1,0:T(8,128)(2,1)} %collective-permute-done.3), channel_id=1, source_target_pairs={{0,1},{1,2},{2,3},{3,4},{4,5},{5,6},{6,7},{7,0},{8,9},{9,10},{10,1... | collective-permute-start | bytes 2949128 | tf_op jit(solution)/shard_map/ppermute | solution.py:94
  62.9 1.2 copy-start.3
  64.6 26.2 %collective-permute-start.4 = (bf16[15,128,256]{2,1,0:T(8,128)(2,1)}, bf16[15,128,256]{2,1,0:T(8,128)(2,1)S(1)}, u32[]{:S(2)}, u32[]{:S(2)}) collective-permute-start(bf16[15,128,256]{2,1,0:T(8,128)(2,1)} %collective-permute-done.2), channel_id=1, source_target_pairs={{0,7},{1,0},{2,1},{3,2},{4,3},{5,4},{6,5},{7,6},{8,15},{9,8},{10,9... | collective-permute-start | bytes 2949128 | tf_op jit(solution)/shard_map/ppermute | solution.py:96
  83.8 23.7 %collective-permute-start.6 = (bf16[15,128,256]{2,1,0:T(8,128)(2,1)}, bf16[15,128,256]{2,1,0:T(8,128)(2,1)S(1)}, u32[]{:S(2)}, u32[]{:S(2)}) collective-permute-start(bf16[15,128,256]{2,1,0:T(8,128)(2,1)} %collective-permute-done.5), channel_id=1, source_target_pairs={{0,1},{1,2},{2,3},{3,4},{4,5},{5,6},{6,7},{7,0},{8,9},{9,10},{10,1... | collective-permute-start | bytes 2949128 | tf_op jit(solution)/shard_map/ppermute | solution.py:94
  115.4 14.3 %copy-start.4 = (s32[960]{0:T(1024)S(1)}, s32[960]{0:T(1024)}, u32[]{:S(2)}) copy-start(s32[960]{0:T(1024)} %param.14) | copy-start | bytes 11524
  115.4 14.3 %copy-start.5 = (s32[960]{0:T(1024)S(1)}, s32[960]{0:T(1024)}, u32[]{:S(2)}) copy-start(s32[960]{0:T(1024)} %param.13) | copy-start | bytes 11524
  115.4 109.0 %all-to-all-start = ((bf16[64,128,256]{2,1,0:T(8,128)(2,1)}), bf16[64,128,256]{2,1,0:T(8,128)(2,1)}, u32[]{:S(2)}, u32[]{:S(2)}) async-start(bf16[64,128,256]{2,1,0:T(8,128)(2,1)} %copy.65), calls=%async_computation | async-start | bytes 8388608 | tf_op jit(solution)/shard_map/all_to_all | solution.py:114
  129.7 97.8 %copy-start.7 = (f32[256,8]{0,1:T(8,128)S(1)}, f32[256,8]{0,1:T(8,128)}, u32[]{:S(2)}) copy-start(f32[256,8]{0,1:T(8,128)} %param.12) | copy-start | bytes 24580
  129.7 97.8 %copy-start.8 = (f32[256]{0:T(256)S(1)}, f32[256]{0:T(256)}, u32[]{:S(2)}) copy-start(f32[256]{0:T(256)} %param.11) | copy-start | bytes 3076
  130.3 102.6 %copy-start.6 = (s32[384]{0:T(512)S(1)}, s32[384]{0:T(512)}, u32[]{:S(2)}) copy-start(s32[384]{0:T(512)} %param.15) | copy-start | bytes 4612
  229.2 15.3 %all-to-all-start.1 = ((f32[8,1,11520]{2,1,0:T(1,128)}), f32[8,1,11520]{2,1,0:T(1,128)S(1)}, u32[]{:S(2)}, u32[]{:S(2)}) async-start(f32[8,1,11520]{2,1,0:T(1,128)} %broadcast_in_dim.89), calls=%async_computation.1 | async-start | bytes 737280 | tf_op jit(solution)/shard_map/all_to_all | solution.py:13
  246.5 22.5 %all-to-all-start.2 = ((f32[64,6,8]{2,1,0:T(8,128)}), f32[64,6,8]{2,1,0:T(8,128)S(1)}, u32[]{:S(2)}, u32[]{:S(2)}) async-start(f32[64,6,8]{2,1,0:T(8,128)} %copy.68), calls=%async_computation.2 | async-start | bytes 524288 | tf_op jit(solution)/shard_map/all_to_all | solution.py:36
